TPU v7x, 32 devices: a whole 2x2x4 slice. The times are simulated.
32 devices in a mesh: rep: 8 (over z, y), shard: 4 (over x, core).
Axes of the slice: x: 2, y: 2, z: 4, core: 2. Of those that a mesh axis runs over, the one named last changes fastest.
Arguments:
- activ: bfloat16 [4096, 8192], P(('rep', 'shard')), may hold values from -6 to 6
- key_grad: bfloat16 [4096, 640], P(('rep', 'shard')), may hold values from -1.1953125 to 1.1953125
- key_weight: bfloat16 [8192, 640], P('shard'), may hold values from -0.25 to 0.25
- feedback: bfloat16 [8, 40960, 128], P('rep', 'shard'), may hold values from -24 to 24
- kept: int32 [8, 4, 512], P('rep', 'shard'), may hold values from 0 to 10239, as said below
- region_len: int32 [4, 8], P('shard'), may hold values from 640 to 1920, as said below
Outputs:
- input_grad: bfloat16 [4096, 8192], P(('rep', 'shard'))
- next_feedback: bfloat16 [8, 40960, 128], P('rep', 'shard')
- owned_sum: float32 [4, 15360, 128], P('shard', 'rep')
Inputs may be any that keep to these rules, and one draw needn't show every extreme that they name: `region_len`: each row splits its shard's 10240 blocks into 8 regions in order of owner and sums to 10240; every row has a region of exactly 1920 blocks. `kept`: the 512 numbers of a row are different blocks of that shard. At most 128 of them lie in one region of the shard; every row has exactly 128 in some region, and in every shard some region gets exactly 128 from every replica.
All inputs are finite; a program needn't handle non-finite values.
Results may differ from a plain program's by a relative error of at most 0.011.
Values may be sent and summed in bfloat16 or wider, within the bound.
A program may use at most 128 MiB of HBM per device.

v0:
```python
import jax
import jax.numpy as jnp
from jax import lax
from jax.sharding import PartitionSpec as P


def accumulate(block_rows, block_ids, own_start, own_len, region_max):
    offset = block_ids - own_start
    inside = (offset >= 0) & (offset < own_len)
    target = jnp.where(inside, offset, region_max)
    blank = jnp.zeros((region_max, block_rows.shape[1]), jnp.float32)
    return blank.at[target].add(block_rows.astype(jnp.float32), mode="drop")


def per_device(activ, key_grad, key_weight, feedback, kept, region_len):
    grads_all = lax.all_gather(key_grad, "shard", axis=0, tiled=True)
    act_cols = lax.all_to_all(activ, "shard", split_axis=1, concat_axis=0, tiled=True)
    weight_grad = lax.dot_general(
        act_cols, grads_all, (((0,), (0,)), ((), ())), preferred_element_type=jnp.float32
    )
    input_cols = lax.dot_general(
        grads_all, key_weight, (((1,), (1,)), ((), ())), preferred_element_type=jnp.float32
    ).astype(jnp.bfloat16)
    input_grad = lax.all_to_all(input_cols, "shard", split_axis=0, concat_axis=1, tiled=True)
    table = feedback[0]
    chosen = kept[0, 0]
    lengths = region_len[0]
    replicas = lax.axis_size("rep")
    block_count = table.shape[0]
    block_size = table.shape[1]
    keep_count = chosen.shape[0]
    mean_len = block_count // replicas
    region_max = mean_len + mean_len // 2
    starts = jnp.cumsum(lengths) - lengths
    owner_self = lax.axis_index("rep")
    own_start = starts[owner_self]
    own_len = lengths[owner_self]
    kept_rows = table[chosen]
    flags = jnp.zeros((block_count,), bool).at[chosen].set(True)
    cleared = jnp.where(flags[:, None], jnp.float32(0.0), table.astype(jnp.float32))
    next_feedback = (cleared + weight_grad.reshape(block_count, block_size)).astype(jnp.bfloat16)[
        None
    ]
    owner_id = jnp.sum((starts[None, :] <= chosen[:, None]).astype(jnp.int32), axis=1) - 1
    serial = jnp.arange(keep_count, dtype=jnp.int32)
    earlier = (owner_id[:, None] == owner_id[None, :]) & (serial[None, :] < serial[:, None])
    slot_index = jnp.sum(earlier.astype(jnp.int32), axis=1)
    capacity = 2 * keep_count // replicas
    place_at = owner_id * capacity + slot_index
    send_rows = (
        jnp.zeros((replicas * capacity, block_size), jnp.bfloat16).at[place_at].set(kept_rows)
    )
    send_ids = jnp.full((replicas * capacity,), -1, jnp.int32).at[place_at].set(chosen)
    got_rows, got_ids = (
        lax.all_to_all(send_rows, "rep", split_axis=0, concat_axis=0, tiled=True),
        lax.all_to_all(send_ids, "rep", split_axis=0, concat_axis=0, tiled=True),
    )
    owned_rows = accumulate(got_rows, got_ids, own_start, own_len, region_max)
    return (input_grad, next_feedback, owned_rows[None])


def solution(mesh):
    return jax.shard_map(
        per_device,
        mesh=mesh,
        in_specs=(
            P(("rep", "shard"), None),
            P(("rep", "shard"), None),
            P("shard", None),
            P("rep", "shard", None),
            P("rep", "shard", None),
            P("shard", None),
        ),
        out_specs=(P(("rep", "shard"), None), P("rep", "shard", None), P("shard", "rep", None)),
        check_vma=False,
    )
```

profile of v0, /device:TPU:0, one launch (start us, length us, event | category | flops | bytes accessed | tf_op | source)
XLA Modules:
  0.0 117.7 jit_solution(1622688939139694994)
XLA Ops:
  0.6 0.0 copy-start
  0.6 1.0 reduce-window.4
  1.6 0.7 fusion.11
  2.3 0.8 convert_reduce_fusion.1
  3.1 0.3 convert_reduce_fusion
  3.3 3.2 %scatter_custom_fusion.1 = s32[1024]{0:T(1024)} fusion(s32[512]{0:T(512)S(1)} %bitcast.56, s32[512]{0:T(512)} %bitcast.54, s32[]{:T(128)} %constant.18.clone.1), kind=kCustom, calls=%fused_computation.26 | custom fusion | bytes 4608 | tf_op jit(solution)/shard_map/scatter | solution.py:53
  6.5 7.3 %all-to-all-start.2 = ((s32[8,128,1]{1,2,0:T(1,128)}), s32[8,128,1]{1,2,0:T(1,128)S(1)}, u32[]{:S(2)}, u32[]{:S(2)}) async-start(s32[8,128,1]{1,2,0:T(1,128)} %bitcast.14), calls=%async_computation.2 | async-start | bytes 8192 | tf_op jit(solution)/shard_map/all_to_all | solution.py:56
  13.8 0.7 compare_select_fusion.2
  14.5 0.0 copy-start.2
  14.5 0.6 copy-done.2
  15.1 5.5 %scatter_custom_fusion.2 = bf16[1024,128]{1,0:T(8,128)(2,1)} fusion(s32[512]{0:T(512)S(1)} %bitcast.57, bf16[]{:T(256)} %constant.12.clone.1, bf16[10240,128]{1,0:T(8,128)(2,1)} %bitcast.43, s32[1024]{0:T(1024)S(1)} %pad_clamp_fusion), kind=kCustom, calls=%fused_computation.13 | custom fusion | bytes 262656 | tf_op jit(solution)/shard_map/scatter | solution.py:51
  20.6 0.0 all-to-all-done.2
  20.6 6.0 %all-to-all-start.3 = ((bf16[8,128,128]{2,1,0:T(8,128)(2,1)}), bf16[8,128,128]{2,1,0:T(8,128)(2,1)S(1)}, u32[]{:S(2)}, u32[]{:S(2)}) async-start(bf16[8,128,128]{2,1,0:T(8,128)(2,1)} %bitcast.23), calls=%async_computation.3 | async-start | bytes 524288 | tf_op jit(solution)/shard_map/all_to_all | solution.py:55
  26.6 4.1 %copy.20 = bf16[128,8192]{0,1:T(8,128)(2,1)} copy(bf16[128,8192]{1,0:T(8,128)(2,1)} %param.6) | data formatting | bytes 4194304 | tf_op args[0]
  30.7 4.4 %all-to-all-done.3 = bf16[8,128,128]{2,1,0:T(8,128)(2,1)S(1)} async-done(((bf16[8,128,128]{2,1,0:T(8,128)(2,1)}), bf16[8,128,128]{2,1,0:T(8,128)(2,1)S(1)}, u32[]{:S(2)}, u32[]{:S(2)}) %all-to-all-start.3) | async-done | bytes 262176 | tf_op jit(solution)/shard_map/all_to_all | solution.py:55
  35.1 4.4 %all-to-all-start.1 = ((bf16[128,4,2048]{0,2,1:T(8,128)(2,1)}), bf16[128,4,2048]{0,2,1:T(8,128)(2,1)}, u32[]{:S(2)}, u32[]{:S(2)}) async-start(bf16[128,4,2048]{0,2,1:T(8,128)(2,1)} %bitcast.42), calls=%async_computation.1 | async-start | bytes 4194304 | tf_op jit(solution)/shard_map/all_to_all | solution.py:17
  39.6 30.0 %all_gather.3 = bf16[512,640]{1,0:T(8,128)(2,1)S(1)} all-gather(bf16[128,640]{1,0:T(8,128)(2,1)} %param.7), channel_id=1, replica_groups=mesh['rep'=8,'shard'=4] {'shard'}, dimensions={0}, use_global_device_ids=true | all-gather | bytes 819200 | tf_op jit(solution)/shard_map/all_gather | solution.py:16
  69.6 0.0 copy-done
  69.6 3.1 %convolution_convert_fusion = bf16[512,2048]{1,0:T(8,128)(2,1)} fusion(bf16[512,640]{1,0:T(8,128)(2,1)S(1)} %all_gather.3, bf16[2048,640]{1,0:T(8,128)(2,1)S(1)} %copy-done), kind=kOutput, calls=%fused_computation.6 | convolution fusion | flops 1343225856 | bytes 5373952 | tf_op jit(solution)/shard_map/dot_general | solution.py:21
  72.7 0.0 copy-start.3
  72.7 0.0 all-to-all-done.1
  72.7 4.6 %all-to-all-start = ((bf16[4,128,2048]{2,1,0:T(8,128)(2,1)}), bf16[4,128,2048]{2,1,0:T(8,128)(2,1)}, u32[]{:S(2)}, u32[]{:S(2)}) async-start(bf16[4,128,2048]{2,1,0:T(8,128)(2,1)} %bitcast.44), calls=%async_computation | async-start | bytes 4194304 | tf_op jit(solution)/shard_map/all_to_all | solution.py:24
  77.4 0.0 copy-done.3
  77.4 0.6 constant_dynamic-slice_fusion
  78.0 0.6 dynamic_slice.6
  78.6 0.5 broadcast.121
  79.1 2.6 %scatter_custom_fusion = pred[10240]{0:T(1024)(128)(4,1)S(1)} fusion(s32[512]{0:T(512)} %bitcast.51, pred[512]{0:T(512)(128)(4,1)} %broadcast.121, pred[]{:T(512)} %constant.13.clone.1), kind=kCustom, calls=%fused_computation.17 | custom fusion | bytes 10752 | tf_op jit(solution)/shard_map/scatter | solution.py:39
  81.7 0.7 broadcast_subtract_fusion
  82.3 0.6 compare_select_fusion
  83.0 7.0 %scatter_custom_fusion.3 = f32[1920,128]{1,0:T(8,128)} fusion(s32[1024]{0:T(1024)S(1)} %bitcast.55, bf16[1024,128]{1,0:T(8,128)(2,1)S(1)} %bitcast.46, f32[]{:T(128)} %constant.17.clone.1), kind=kCustom, calls=%fused_computation.10 | custom fusion | flops 262144 | bytes 1245188 | tf_op jit(solution)/shard_map/scatter-add | solution.py:12
  90.0 3.9 %copy.21 = bf16[4,128,2048]{2,1,0:T(8,128)(2,1)} copy(bf16[4,128,2048]{1,2,0:T(8,128)(2,1)} %bitcast.5) | data formatting | bytes 4194304 | tf_op jit(solution)/shard_map/all_to_all | solution.py:17
  93.9 5.8 %fusion.12 = f32[2048,640]{1,0:T(8,128)} fusion(bf16[512,2048]{1,0:T(8,128)(2,1)} %bitcast.41, bf16[512,640]{1,0:T(8,128)(2,1)S(1)} %all_gather.3), kind=kOutput, calls=%fused_computation.33 | convolution fusion | flops 1342177280 | bytes 7995392 | tf_op jit(solution)/shard_map/dot_general | solution.py:18
  99.7 6.5 %reshape.138 = f32[1,10240,128]{2,1,0:T(8,128)} reshape(f32[2048,640]{1,0:T(8,128)} %fusion.12) | data formatting | bytes 10485760 | tf_op jit(solution)/shard_map/reshape | solution.py:41
  106.2 0.0 all-to-all-done
  106.2 0.0 copy-start.1
  106.2 3.3 %copy.24 = bf16[4,16,8,2048]{3,2,0,1:T(8,128)(2,1)} copy(bf16[4,16,8,2048]{3,2,1,0:T(8,128)(2,1)} %bitcast.28) | data formatting | bytes 4194304 | tf_op jit(solution)/shard_map/all_to_all | solution.py:24
  109.5 0.0 copy-done.1
  109.5 8.2 %add_convert_fusion = bf16[1,10240,128]{2,1,0:T(8,128)(2,1)} fusion(f32[1,10240,128]{2,1,0:T(8,128)} %reshape.138, bf16[1,10240,128]{2,1,0:T(8,128)(2,1)S(1)} %copy-done.1, pred[10240]{0:T(1024)(128)(4,1)S(1)} %scatter_custom_fusion), kind=kLoop, calls=%fused_computation.5 | loop fusion | flops 5242880 | bytes 10496000 | tf_op jit(solution)/shard_map/convert_element_type | solution.py:41
  (5 shorter events, 0.0 us)
Async XLA Ops:
  0.6 68.9 %copy-start = (bf16[2048,640]{1,0:T(8,128)(2,1)S(1)}, bf16[2048,640]{1,0:T(8,128)(2,1)}, u32[]{:S(2)}) copy-start(bf16[2048,640]{1,0:T(8,128)(2,1)} %param.8) | copy-start | bytes 7864324
  6.5 14.1 %all-to-all-start.2 = ((s32[8,128,1]{1,2,0:T(1,128)}), s32[8,128,1]{1,2,0:T(1,128)S(1)}, u32[]{:S(2)}, u32[]{:S(2)}) async-start(s32[8,128,1]{1,2,0:T(1,128)} %bitcast.14), calls=%async_computation.2 | async-start | bytes 8192 | tf_op jit(solution)/shard_map/all_to_all | solution.py:56
  14.5 0.6 copy-start.2
  20.6 14.5 %all-to-all-start.3 = ((bf16[8,128,128]{2,1,0:T(8,128)(2,1)}), bf16[8,128,128]{2,1,0:T(8,128)(2,1)S(1)}, u32[]{:S(2)}, u32[]{:S(2)}) async-start(bf16[8,128,128]{2,1,0:T(8,128)(2,1)} %bitcast.23), calls=%async_computation.3 | async-start | bytes 524288 | tf_op jit(solution)/shard_map/all_to_all | solution.py:55
  35.1 37.6 %all-to-all-start.1 = ((bf16[128,4,2048]{0,2,1:T(8,128)(2,1)}), bf16[128,4,2048]{0,2,1:T(8,128)(2,1)}, u32[]{:S(2)}, u32[]{:S(2)}) async-start(bf16[128,4,2048]{0,2,1:T(8,128)(2,1)} %bitcast.42), calls=%async_computation.1 | async-start | bytes 4194304 | tf_op jit(solution)/shard_map/all_to_all | solution.py:17
  72.7 4.6 %copy-start.3 = (s32[1,8]{1,0:T(1,128)S(1)}, s32[1,8]{1,0:T(1,128)}, u32[]{:S(2)}) copy-start(s32[1,8]{1,0:T(1,128)} %param.11) | copy-start | bytes 100
  72.7 33.5 %all-to-all-start = ((bf16[4,128,2048]{2,1,0:T(8,128)(2,1)}), bf16[4,128,2048]{2,1,0:T(8,128)(2,1)}, u32[]{:S(2)}, u32[]{:S(2)}) async-start(bf16[4,128,2048]{2,1,0:T(8,128)(2,1)} %bitcast.44), calls=%async_computation | async-start | bytes 4194304 | tf_op jit(solution)/shard_map/all_to_all | solution.py:24
  106.2 3.3 %copy-start.1 = (bf16[1,10240,128]{2,1,0:T(8,128)(2,1)S(1)}, bf16[1,10240,128]{2,1,0:T(8,128)(2,1)}, u32[]{:S(2)}) copy-start(bf16[1,10240,128]{2,1,0:T(8,128)(2,1)} %param.9) | copy-start | bytes 7864324
where the time goes:
time: 119 us; the launch traced here: 118 us
  local copies, waits for them, and re-layouts  31.4 us (26%)
  blocking collectives  30 us (25%)
  starting transfers between devices  22.4 us (19%)
  other arithmetic  19.8 us (17%)
  matrix products  8.92 us (7%)
  waiting for transfers between devices  4.45 us (4%)
    all_gather x1, blocking collectives, per_device(): grads_all = lax.all_gather(key_grad, 'shard', axis=0, tiled=True)  30 us
    convert_element_type x1, other arithmetic, per_device(): (cleared + weight_grad.reshape(block_count, block_size)).astype(jnp.bfloa...  8.16 us
    all_to_all x1, starting transfers between devices, per_device(): lax.all_to_all(send_ids, 'rep', split_axis=0, concat_axis=0, tiled=True)  7.31 us
    scatter-add x1, other arithmetic, accumulate(): return blank.at[target].add(block_rows.astype(jnp.float32), mode='drop')  7.02 us
    reshape x1, local copies, waits for them, and re-layouts, per_device(): weight_grad.reshape(block_count, block_size)  6.47 us
    all_to_all x1, starting transfers between devices, per_device(): lax.all_to_all(send_rows, 'rep', split_axis=0, concat_axis=0, tiled=True)  6 us
    dot_general x1, matrix products, per_device(): lax.dot_general(act_cols, grads_all, (((0,), (0,)), ((), ())), preferred_...  5.78 us
    scatter x1, local copies, waits for them, and re-layouts, per_device(): jnp.zeros((replicas * capacity, block_size), jnp.bfloat16).at[place_at]  5.51 us
  transfers between devices with their start and end apart: 4, of which 1 were waited for; matrix products, arithmetic and copies ran while one was open for 36% of the time, Pallas kernels for 0%

commit v1 on v0

--- a/solution.py
+++ b/solution.py
@@ -2,6 +2,19 @@
 import jax.numpy as jnp
 from jax import lax
 from jax.sharding import PartitionSpec as P
+
+
+def plan_levels_all(packet):
+    amount_of = lax.psum(1, "shard")
+    block_out = sorted(((src_i, (src_i + 1) % amount_of) for src_i in range(amount_of)))
+    built = packet
+    seen = [built]
+    for p in [*range(1, amount_of)]:
+        built = lax.ppermute(built, "shard", block_out)
+        seen.insert(0, built)
+    piece_out = jnp.concatenate(seen, 0)
+    passed = jnp.roll(piece_out, (lax.axis_index("shard") + 1) * packet.shape[0], 0)
+    return passed
 
 
 def accumulate(block_rows, block_ids, own_start, own_len, region_max):
@@ -13,7 +26,7 @@
 
 
 def per_device(activ, key_grad, key_weight, feedback, kept, region_len):
-    grads_all = lax.all_gather(key_grad, "shard", axis=0, tiled=True)
+    grads_all = plan_levels_all(key_grad)
     act_cols = lax.all_to_all(activ, "shard", split_axis=1, concat_axis=0, tiled=True)
     weight_grad = lax.dot_general(
         act_cols, grads_all, (((0,), (0,)), ((), ())), preferred_element_type=jnp.float32

time: 119 us -> 111 us (0.933)
  blocking collectives: 30 us -> 0 us
  waiting for transfers between devices: 4.45 us -> 18.7 us
  local copies, waits for them, and re-layouts: 31.4 us -> 37.2 us
  starting transfers between devices: 22.4 us -> 24.3 us
    all_gather x1 -> x0, blocking collectives: 30 us -> none  [per_device(): grads_all = lax.all_gather(key_grad, 'shard', axis=0, tiled=True)]
    ppermute x0 -> x3, waiting for transfers between devices: none -> 18.5 us  [plan_levels_all(): built = lax.ppermute(built, 'shard', block_out)]
    dot_general x0 -> x1, local copies, waits for them, and re-layouts: none -> 5.96 us  [per_device(): lax.dot_general(act_cols, grads_all, (((0,), (0,)), ((), ())), preferred_...]
    all_to_all x1, waiting for transfers between devices: 4.44 us -> 0.01 us  [per_device(): lax.all_to_all(send_rows, 'rep', split_axis=0, concat_axis=0, tiled=True)]
    ppermute x0 -> x3, starting transfers between devices: none -> 2.12 us  [plan_levels_all(): built = lax.ppermute(built, 'shard', block_out)]
    unnamed x9 -> x16, local copies, waits for them, and re-layouts: 4.68 us -> 5.34 us
  transfers between devices with their start and end apart: 4 -> 7, of which waited for: 1 -> 2; matrix products, arithmetic and copies ran while one was open for 36% -> 51% of each run, Pallas kernels for 0% -> 0%
where the time goes in v1:
time: 111 us; the launch traced here: 110 us
  local copies, waits for them, and re-layouts  37.2 us (34%)
  starting transfers between devices  24.3 us (22%)
  other arithmetic  20.3 us (18%)
  waiting for transfers between devices  18.7 us (17%)
  matrix products  8.88 us (8%)
    ppermute x3, waiting for transfers between devices, plan_levels_all(): built = lax.ppermute(built, 'shard', block_out)  18.5 us
    convert_element_type x1, other arithmetic, per_device(): (cleared + weight_grad.reshape(block_count, block_size)).astype(jnp.bfloa...  8.55 us
    all_to_all x1, starting transfers between devices, per_device(): lax.all_to_all(send_ids, 'rep', split_axis=0, concat_axis=0, tiled=True)  7.31 us
    scatter-add x1, other arithmetic, accumulate(): return blank.at[target].add(block_rows.astype(jnp.float32), mode='drop')  7.02 us
    reshape x1, local copies, waits for them, and re-layouts, per_device(): weight_grad.reshape(block_count, block_size)  6.47 us
    dot_general x1, local copies, waits for them, and re-layouts, per_device(): lax.dot_general(act_cols, grads_all, (((0,), (0,)), ((), ())), preferred_...  5.96 us
    all_to_all x1, starting transfers between devices, per_device(): lax.all_to_all(send_rows, 'rep', split_axis=0, concat_axis=0, tiled=True)  5.79 us
    dot_general x1, matrix products, per_device(): lax.dot_general(act_cols, grads_all, (((0,), (0,)), ((), ())), preferred_...  5.67 us
  transfers between devices with their start and end apart: 7, of which 2 were waited for; matrix products, arithmetic and copies ran while one was open for 51% of the time, Pallas kernels for 0%

profile of v1, /device:TPU:0, one launch (start us, length us, event | category | flops | bytes accessed | tf_op | source)
XLA Modules:
  0.0 110.2 jit_solution(6701992643124041882)
XLA Ops:
  0.6 0.0 copy-start
  0.6 1.0 reduce-window.4
  1.6 0.7 fusion.13
  2.3 0.8 convert_reduce_fusion.1
  3.1 0.3 convert_reduce_fusion
  3.3 3.2 %scatter_custom_fusion.1 = s32[1024]{0:T(1024)} fusion(s32[512]{0:T(512)S(1)} %bitcast.56, s32[512]{0:T(512)} %bitcast.54, s32[]{:T(128)} %constant.58.clone.1), kind=kCustom, calls=%fused_computation.37 | custom fusion | bytes 4608 | tf_op jit(solution)/shard_map/scatter | solution.py:66
  6.5 7.3 %all-to-all-start.2 = ((s32[8,128,1]{1,2,0:T(1,128)}), s32[8,128,1]{1,2,0:T(1,128)S(1)}, u32[]{:S(2)}, u32[]{:S(2)}) async-start(s32[8,128,1]{1,2,0:T(1,128)} %bitcast.15), calls=%async_computation.2 | async-start | bytes 8192 | tf_op jit(solution)/shard_map/all_to_all | solution.py:69
  13.8 0.7 compare_select_fusion.2
  14.5 5.5 %scatter_custom_fusion.2 = bf16[1024,128]{1,0:T(8,128)(2,1)} fusion(s32[512]{0:T(512)S(1)} %bitcast.57, bf16[]{:T(256)} %constant.64.clone.1, bf16[10240,128]{1,0:T(8,128)(2,1)} %bitcast.43, s32[1024]{0:T(1024)S(1)} %pad_clamp_fusion), kind=kCustom, calls=%fused_computation.16 | custom fusion | bytes 262656 | tf_op jit(solution)/shard_map/scatter | solution.py:64
  20.0 0.2 all-to-all-done.2
  20.2 5.8 %all-to-all-start.3 = ((bf16[8,128,128]{2,1,0:T(8,128)(2,1)}), bf16[8,128,128]{2,1,0:T(8,128)(2,1)S(1)}, u32[]{:S(2)}, u32[]{:S(2)}) async-start(bf16[8,128,128]{2,1,0:T(8,128)(2,1)} %bitcast.24), calls=%async_computation.3 | async-start | bytes 524288 | tf_op jit(solution)/shard_map/all_to_all | solution.py:68
  26.0 0.0 collective-permute-start
  26.0 0.0 copy-start.3
  26.1 4.1 %copy.23 = bf16[128,8192]{0,1:T(8,128)(2,1)} copy(bf16[128,8192]{1,0:T(8,128)(2,1)} %param.6) | data formatting | bytes 4194304 | tf_op args[0]
  30.1 0.0 copy-done.3
  30.1 0.6 constant_dynamic-slice_fusion
  30.7 0.6 dynamic_slice.11
  31.3 2.5 %scatter_custom_fusion = pred[10240]{0:T(1024)(128)(4,1)S(1)} fusion(s32[512]{0:T(512)S(1)} %bitcast.51, pred[512]{0:T(512)(128)(4,1)S(1)} %broadcast.122, pred[]{:T(512)} %constant.54.clone.1), kind=kCustom, calls=%fused_computation.20 | custom fusion | bytes 10241 | tf_op jit(solution)/shard_map/scatter | solution.py:52
  33.8 0.0 collective-permute-done
  33.8 1.6 %collective-permute-start.1 = (bf16[128,640]{1,0:T(8,128)(2,1)S(1)}, bf16[128,640]{1,0:T(8,128)(2,1)S(1)}, u32[]{:S(2)}, u32[]{:S(2)}) collective-permute-start(bf16[128,640]{1,0:T(8,128)(2,1)S(1)} %collective-permute-done), channel_id=1, source_target_pairs={{0,1},{1,2},{2,3},{3,0},{4,5},{5,6},{6,7},{7,4},{8,9},{9,10},{10,1... | collective-permute-start | bytes 491528 | tf_op jit(solution)/shard_map/ppermute | solution.py:13
  35.4 0.0 all-to-all-done.3
  35.4 4.4 %all-to-all-start.1 = ((bf16[128,4,2048]{0,2,1:T(8,128)(2,1)}), bf16[128,4,2048]{0,2,1:T(8,128)(2,1)}, u32[]{:S(2)}, u32[]{:S(2)}) async-start(bf16[128,4,2048]{0,2,1:T(8,128)(2,1)} %bitcast.42), calls=%async_computation.1 | async-start | bytes 4194304 | tf_op jit(solution)/shard_map/all_to_all | solution.py:30
  39.9 0.0 copy-start.1
  39.9 0.7 broadcast_subtract_fusion
  40.6 0.0 collective-permute-done.1
  40.6 0.5 collective-permute-start.2
  41.1 0.6 compare_select_fusion
  41.7 7.0 %scatter_custom_fusion.3 = f32[1920,128]{1,0:T(8,128)} fusion(s32[1024]{0:T(1024)S(1)} %bitcast.55, bf16[1024,128]{1,0:T(8,128)(2,1)S(1)} %bitcast.46, f32[]{:T(128)} %constant.57.clone.1), kind=kCustom, calls=%fused_computation.13 | custom fusion | flops 262144 | bytes 1245188 | tf_op jit(solution)/shard_map/scatter-add | solution.py:25
  48.7 18.5 %collective-permute-done.2 = bf16[128,640]{1,0:T(8,128)(2,1)S(1)} collective-permute-done((bf16[128,640]{1,0:T(8,128)(2,1)S(1)}, bf16[128,640]{1,0:T(8,128)(2,1)S(1)}, u32[]{:S(2)}, u32[]{:S(2)}) %collective-permute-start.2) | collective-permute-done | bytes 163872 | tf_op jit(solution)/shard_map/ppermute | solution.py:13
  67.3 0.0 copy-done.1
  67.5 0.0 copy-start.2
  67.5 1.1 copy-done.2
  68.6 0.0 copy-done
  68.6 3.2 %convolution_convert_fusion = bf16[512,2048]{1,0:T(8,128)(2,1)} fusion(bf16[2048,640]{1,0:T(8,128)(2,1)S(1)} %copy-done, bf16[1024,640]{1,0:T(8,128)(2,1)S(1)} %constant_dynamic-update-slice_fusion, s32[]{:T(128)S(6)} %select_n.66), kind=kOutput, calls=%fused_computation.7 | convolution fusion | flops 1343225856 | bytes 5373956 | tf_op jit(solution)/shard_map/dot_general | solution.py:34
  71.8 0.0 all-to-all-done.1
  71.8 4.7 %all-to-all-start = ((bf16[4,128,2048]{2,1,0:T(8,128)(2,1)}), bf16[4,128,2048]{2,1,0:T(8,128)(2,1)}, u32[]{:S(2)}, u32[]{:S(2)}) async-start(bf16[4,128,2048]{2,1,0:T(8,128)(2,1)} %bitcast.44), calls=%async_computation | async-start | bytes 4194304 | tf_op jit(solution)/shard_map/all_to_all | solution.py:37
  76.5 4.0 %copy.24 = bf16[4,128,2048]{2,1,0:T(8,128)(2,1)} copy(bf16[4,128,2048]{1,2,0:T(8,128)(2,1)} %bitcast.5) | data formatting | bytes 4194304 | tf_op jit(solution)/shard_map/all_to_all | solution.py:30
  80.4 5.7 %convolution_bitcast_fusion = f32[2048,640]{0,1:T(8,128)} fusion(bf16[512,2048]{1,0:T(8,128)(2,1)} %bitcast.41, bf16[1024,640]{1,0:T(8,128)(2,1)} %copy-done.2, s32[]{:T(128)S(6)} %select_n.66), kind=kOutput, calls=%fused_computation.6 | convolution fusion | flops 1342177280 | bytes 7995396 | tf_op jit(solution)/shard_map/dot_general | solution.py:31
  86.1 6.0 %copy.25 = f32[2048,640]{1,0:T(8,128)} copy(f32[2048,640]{0,1:T(8,128)} %convolution_bitcast_fusion) | data formatting | bytes 10485760 | tf_op jit(solution)/shard_map/dot_general | solution.py:31
  92.1 6.5 %reshape.138 = f32[1,10240,128]{2,1,0:T(8,128)} reshape(f32[2048,640]{1,0:T(8,128)} %copy.25) | data formatting | bytes 10485760 | tf_op jit(solution)/shard_map/reshape | solution.py:54
  98.5 8.5 %add_convert_fusion = bf16[1,10240,128]{2,1,0:T(8,128)(2,1)} fusion(f32[1,10240,128]{2,1,0:T(8,128)} %reshape.138, bf16[1,10240,128]{2,1,0:T(8,128)(2,1)} %param.9, pred[10240]{0:T(1024)(128)(4,1)S(1)} %scatter_custom_fusion), kind=kLoop, calls=%fused_computation.5 | loop fusion | flops 5242880 | bytes 10496000 | tf_op jit(solution)/shard_map/convert_element_type | solution.py:54
  107.1 0.0 all-to-all-done
  107.1 3.2 %copy.28 = bf16[4,16,8,2048]{3,2,0,1:T(8,128)(2,1)} copy(bf16[4,16,8,2048]{3,2,1,0:T(8,128)(2,1)} %bitcast.29) | data formatting | bytes 4194304 | tf_op jit(solution)/shard_map/all_to_all | solution.py:37
  (14 shorter events, 0.2 us)
Async XLA Ops:
  0.6 68.0 %copy-start = (bf16[2048,640]{1,0:T(8,128)(2,1)S(1)}, bf16[2048,640]{1,0:T(8,128)(2,1)}, u32[]{:S(2)}) copy-start(bf16[2048,640]{1,0:T(8,128)(2,1)} %param.8) | copy-start | bytes 7864324
  6.5 13.7 %all-to-all-start.2 = ((s32[8,128,1]{1,2,0:T(1,128)}), s32[8,128,1]{1,2,0:T(1,128)S(1)}, u32[]{:S(2)}, u32[]{:S(2)}) async-start(s32[8,128,1]{1,2,0:T(1,128)} %bitcast.15), calls=%async_computation.2 | async-start | bytes 8192 | tf_op jit(solution)/shard_map/all_to_all | solution.py:69
  20.2 15.2 %all-to-all-start.3 = ((bf16[8,128,128]{2,1,0:T(8,128)(2,1)}), bf16[8,128,128]{2,1,0:T(8,128)(2,1)S(1)}, u32[]{:S(2)}, u32[]{:S(2)}) async-start(bf16[8,128,128]{2,1,0:T(8,128)(2,1)} %bitcast.24), calls=%async_computation.3 | async-start | bytes 524288 | tf_op jit(solution)/shard_map/all_to_all | solution.py:68
  26.0 7.8 %collective-permute-start = (bf16[128,640]{1,0:T(8,128)(2,1)}, bf16[128,640]{1,0:T(8,128)(2,1)S(1)}, u32[]{:S(2)}, u32[]{:S(2)}) collective-permute-start(bf16[128,640]{1,0:T(8,128)(2,1)} %param.7), channel_id=1, source_target_pairs={{0,1},{1,2},{2,3},{3,0},{4,5},{5,6},{6,7},{7,4},{8,9},{9,10},{10,1... | collective-permute-start | bytes 491528 | tf_op jit(solution)/shard_map/ppermute | solution.py:13
  26.0 4.1 %copy-start.3 = (s32[1,8]{1,0:T(1,128)S(1)}, s32[1,8]{1,0:T(1,128)}, u32[]{:S(2)}) copy-start(s32[1,8]{1,0:T(1,128)} %param.11) | copy-start | bytes 100
  33.8 6.8 %collective-permute-start.1 = (bf16[128,640]{1,0:T(8,128)(2,1)S(1)}, bf16[128,640]{1,0:T(8,128)(2,1)S(1)}, u32[]{:S(2)}, u32[]{:S(2)}) collective-permute-start(bf16[128,640]{1,0:T(8,128)(2,1)S(1)} %collective-permute-done), channel_id=1, source_target_pairs={{0,1},{1,2},{2,3},{3,0},{4,5},{5,6},{6,7},{7,4},{8,9},{9,10},{10,1... | collective-permute-start | bytes 491528 | tf_op jit(solution)/shard_map/ppermute | solution.py:13
  35.4 36.4 %all-to-all-start.1 = ((bf16[128,4,2048]{0,2,1:T(8,128)(2,1)}), bf16[128,4,2048]{0,2,1:T(8,128)(2,1)}, u32[]{:S(2)}, u32[]{:S(2)}) async-start(bf16[128,4,2048]{0,2,1:T(8,128)(2,1)} %bitcast.42), calls=%async_computation.1 | async-start | bytes 4194304 | tf_op jit(solution)/shard_map/all_to_all | solution.py:30
  39.9 27.5 %copy-start.1 = (bf16[128,640]{1,0:T(8,128)(2,1)S(1)}, bf16[128,640]{1,0:T(8,128)(2,1)}, u32[]{:S(2)}) copy-start(bf16[128,640]{1,0:T(8,128)(2,1)} %param.7) | copy-start | bytes 491524
  40.6 26.7 %collective-permute-start.2 = (bf16[128,640]{1,0:T(8,128)(2,1)S(1)}, bf16[128,640]{1,0:T(8,128)(2,1)S(1)}, u32[]{:S(2)}, u32[]{:S(2)}) collective-permute-start(bf16[128,640]{1,0:T(8,128)(2,1)S(1)} %collective-permute-done.1), channel_id=1, source_target_pairs={{0,1},{1,2},{2,3},{3,0},{4,5},{5,6},{6,7},{7,4},{8,9},{9,10},{10,1... | collective-permute-start | bytes 491528 | tf_op jit(solution)/shard_map/ppermute | solution.py:13
  67.5 1.1 copy-start.2
  71.8 35.3 %all-to-all-start = ((bf16[4,128,2048]{2,1,0:T(8,128)(2,1)}), bf16[4,128,2048]{2,1,0:T(8,128)(2,1)}, u32[]{:S(2)}, u32[]{:S(2)}) async-start(bf16[4,128,2048]{2,1,0:T(8,128)(2,1)} %bitcast.44), calls=%async_computation | async-start | bytes 4194304 | tf_op jit(solution)/shard_map/all_to_all | solution.py:37
